TPU v7x, 32 devices: a whole 2x2x4 slice. The times are simulated.
32 devices in a mesh: rows: 8 (over z, x), width: 4 (over y, core).
Axes of the slice: x: 2, y: 2, z: 4, core: 2. Of those that a mesh axis runs over, the one named last changes fastest.
Arguments:
- w_gate: float32 [3072, 8192], P('rows', 'width'), may hold values from -0.15625 to 0.15625
- avg_gate: float32 [3072, 8192], P('rows', 'width'), may hold values from -0.109375 to 0.109375
- w_up: float32 [3072, 8192], P('rows', 'width'), may hold values from -0.15625 to 0.15625
- avg_up: float32 [3072, 8192], P('rows', 'width'), may hold values from -0.109375 to 0.109375
- norm_gain: float32 [3072], P('rows'), may hold values from 0.25 to 1.75
Outputs:
- serve_gate: bfloat16 [3072, 8192], P(None, 'width')
- serve_up: bfloat16 [3072, 8192], P(None, 'width')
- factor_gate: float32 [8192], P('width')
- factor_up: float32 [8192], P('width')
All inputs are finite; a program needn't handle non-finite values. Where the computation divides by a largest or mean magnitude, that divisor is 1e-20 or more.
Results may differ from a plain program's by a relative error of at most 0.001.
Values may be sent and summed in bfloat16 or wider, within the bound.
A program may use at most 128 MiB of HBM per device.

v0:
```python
import functools

import jax
import jax.numpy as jnp
from jax import lax
from jax.experimental import pallas as pl
from jax.experimental.pallas import tpu as pltpu
from jax.sharding import PartitionSpec as P

keep_rate = 0.7
MESH = pl.DeviceIdType.MESH
CHUNKS = 4
VMEM_LIMIT = 60 * 2**20


def ring_place(r, n):
    if n % 2:
        return r
    x, z = r % 2, r // 2
    return z + x * (n - 1 - 2 * z)


def ring_row(p, n):
    if n % 2:
        return p
    half = n // 2
    x, k = p // half, p % half
    return 2 * (k + x * (half - 1 - 2 * k)) + x


def serve_kernel(
    n, chunks, gain_ref, wg_ref, ag_ref, wu_ref, au_ref, go_ref, uo_ref, fg_ref, fu_ref,
    w_in, fresh, narrow, gains, part, got, in_sem, max_send, max_recv, send_sem, recv_sem, own_sem,
):
    me = lax.axis_index("rows")
    place = ring_place(me, n)
    nxt = ring_row((place + 1) % n, n)
    prv = ring_row((place + n - 1) % n, n)
    rows, columns = wg_ref.shape
    size = rows // chunks
    outs, to = (go_ref, uo_ref), (nxt, prv)

    loads = []
    for c in range(chunks):
        at = pl.ds(c * size, size)
        for k, (w_ref, avg_ref) in enumerate(((wg_ref, ag_ref), (wu_ref, au_ref))):
            for j, (src, dst) in enumerate(((w_ref, w_in), (avg_ref, fresh))):
                load = pltpu.make_async_copy(src.at[at], dst.at[k, at], in_sem.at[c, k, j])
                load.start()
                loads.append(load)

    barrier = pltpu.get_barrier_semaphore()
    for d in range(1, n):
        pl.semaphore_signal(barrier, inc=1, device_id={"rows": (me + d) % n}, device_id_type=MESH)

    for first in range(0, rows, 128):
        count = min(128, rows - first)
        line = gain_ref[first : first + count].reshape(1, count)
        gains[first : first + count, :] = jnp.broadcast_to(line, (128, count)).T

    tops = [jnp.zeros((8, columns), jnp.float32)] * 2
    for c in range(chunks):
        for k in range(2):
            loads[(c * 2 + k) * 2].wait()
            loads[(c * 2 + k) * 2 + 1].wait()

            def blend(i, top):
                at = pl.ds(pl.multiple_of(c * size + i * 8, 8), 8)
                gain = jnp.tile(gains[at, :], (1, columns // 128))
                value = (keep_rate * fresh[k, at, :] + (1.0 - keep_rate) * w_in[k, at, :]) * gain
                fresh[k, at, :] = value
                return jnp.maximum(top, jnp.abs(value))

            tops[k] = lax.fori_loop(0, size // 8, blend, tops[k])
    for k in range(2):
        part[k : k + 1, :] = jnp.max(tops[k], axis=0, keepdims=True)

    pl.semaphore_wait(barrier, n - 1)
    copies = []
    for d in range(1, n):
        copy = pltpu.make_async_remote_copy(
            src_ref=part,
            dst_ref=got.at[d - 1],
            send_sem=max_send.at[d - 1],
            recv_sem=max_recv.at[d - 1],
            device_id={"rows": (me + d) % n},
            device_id_type=MESH,
        )
        copy.start()
        copies.append(copy)
    for copy in copies:
        copy.wait()
    factor = jnp.maximum(part[...], jnp.max(got[...], axis=0))
    fg_ref[...] = factor[0:1]
    fu_ref[...] = factor[1:2]
    scale = 1.0 / factor

    def here(turn, c):
        owner = ring_row((place + turn) % n, n)
        return pl.ds(pl.multiple_of(owner * rows + c * size, size), size)

    def send(way, step, c, first=False):
        at = here((n - step) if way == 0 else step, c)
        return pltpu.make_async_remote_copy(
            src_ref=narrow.at[way, pl.ds(c * size, size)] if first else outs[way].at[at],
            dst_ref=outs[way].at[at],
            send_sem=send_sem.at[way, step, c],
            recv_sem=recv_sem.at[way, step, c],
            device_id={"rows": to[way]},
            device_id_type=MESH,
        )

    def landed(way, step, c):
        at = here((n - step - 1) if way == 0 else (step + 1), c)
        pltpu.make_async_remote_copy(
            src_ref=outs[way].at[at],
            dst_ref=outs[way].at[at],
            send_sem=send_sem.at[way, step, c],
            recv_sem=recv_sem.at[way, step, c],
            device_id={"rows": to[way]},
            device_id_type=MESH,
        ).wait_recv()

    for c in range(chunks + 1):
        for way in range(2):
            if c < chunks:
                by = jnp.broadcast_to(scale[way : way + 1, :], (16, columns))

                @pl.loop(0, size // 16)
                def _(i):
                    at = pl.ds(pl.multiple_of(c * size + i * 16, 16), 16)
                    narrow[way, at, :] = (fresh[way, at, :] * by).astype(jnp.bfloat16)

            if c:
                send(way, 0, c - 1, True).start()
    own = [
        pltpu.make_async_copy(
            narrow.at[way], outs[way].at[pl.ds(pl.multiple_of(me * rows, rows), rows)], own_sem.at[way]
        )
        for way in range(2)
    ]
    for copy in own:
        copy.start()

    @pl.loop(1, n - 1)
    def _(step):
        for c in range(chunks):
            for way in range(2):
                landed(way, step - 1, c)
                send(way, step, c).start()

    for c in range(chunks):
        for way in range(2):
            landed(way, n - 2, c)

    for copy in own:
        copy.wait()
    for c in range(chunks):
        for way in range(2):
            send(way, 0, c, True).wait_send()

    @pl.loop(1, n - 1)
    def _(step):
        for c in range(chunks):
            for way in range(2):
                send(way, step, c).wait_send()


def serve(w_gate, avg_gate, w_up, avg_up, norm_gain, n):
    rows, columns = w_gate.shape
    chunks = CHUNKS
    while rows % (16 * chunks):
        chunks -= 1
    whole = jax.ShapeDtypeStruct((n * rows, columns), jnp.bfloat16)
    line = jax.ShapeDtypeStruct((1, columns), jnp.float32)
    anywhere = pl.BlockSpec(memory_space=pl.ANY)
    near = pl.BlockSpec(memory_space=pltpu.VMEM)
    return pl.pallas_call(
        functools.partial(serve_kernel, n, chunks),
        out_shape=(whole, whole, line, line),
        in_specs=[near] + [anywhere] * 4,
        out_specs=(anywhere, anywhere, near, near),
        scratch_shapes=[
            pltpu.VMEM((2, rows, columns), jnp.float32),
            pltpu.VMEM((2, rows, columns), jnp.float32),
            pltpu.VMEM((2, rows, columns), jnp.bfloat16),
            pltpu.VMEM((rows, 128), jnp.float32),
            pltpu.VMEM((2, columns), jnp.float32),
            pltpu.VMEM((n - 1, 2, columns), jnp.float32),
            pltpu.SemaphoreType.DMA((chunks, 2, 2)),
            pltpu.SemaphoreType.DMA((n - 1,)),
            pltpu.SemaphoreType.DMA((n - 1,)),
            pltpu.SemaphoreType.DMA((2, n - 1, chunks)),
            pltpu.SemaphoreType.DMA((2, n - 1, chunks)),
            pltpu.SemaphoreType.DMA((2,)),
        ],
        compiler_params=pltpu.CompilerParams(
            collective_id=0, has_side_effects=True, vmem_limit_bytes=VMEM_LIMIT
        ),
        name="serve",
    )(norm_gain, w_gate, avg_gate, w_up, avg_up)


def local(n, w_gate, avg_gate, w_up, avg_up, norm_gain):
    serve_gate, serve_up, factor_gate, factor_up = serve(w_gate, avg_gate, w_up, avg_up, norm_gain, n)
    return (serve_gate, serve_up, factor_gate[0], factor_up[0])


def solution(mesh):
    placed = (P("rows", "width"),) * 4 + (P("rows"),)
    return jax.shard_map(
        functools.partial(local, mesh.shape["rows"]),
        mesh=mesh,
        in_specs=placed,
        out_specs=(P(None, "width"), P(None, "width"), P("width"), P("width")),
        check_vma=False,
    )
```

profile of v0, /device:TPU:0, one launch (start us, length us, event | category | flops | bytes accessed | tf_op | source)
XLA Modules:
  0.0 272.0 jit_solution(16039847958899854879)
XLA Ops:
  0.6 252.5 %serve.1 = (bf16[3072,2048]{1,0:T(8,128)(2,1)}, bf16[3072,2048]{1,0:T(8,128)(2,1)}, f32[1,2048]{1,0:T(1,128)}, f32[1,2048]{1,0:T(1,128)}) custom-call(f32[384]{0:T(512)} %gain_ref.1, f32[384,2048]{1,0:T(8,128)} %wg_ref.1, f32[384,2048]{1,0:T(8,128)} %ag_ref.1, f32[384,2048]{1,0:T(8,128)} %wu_ref.1, f32[384,2048]{1,0:T(8,128)} %au_ref.1), custom_call_target="tpu_custom_call" | custom-call | tf_op jit(solution)/shard_map/serve/pallas_call | solution.py:178
  253.2 0.0 copy-start
  253.2 11.4 %copy.13 = bf16[3072,2048]{1,0:T(8,128)(2,1)} copy(bf16[3072,2048]{1,0:T(8,128)(2,1)} %get-tuple-element.16) | data formatting | bytes 25165824
  264.5 1.5 copy-done
  266.1 0.0 copy-start.2
  266.1 0.0 copy-start.1
  266.1 4.8 %copy.14 = bf16[3072,2048]{1,0:T(8,128)(2,1)} copy(bf16[3072,2048]{1,0:T(8,128)(2,1)S(1)} %copy-done) | data formatting | bytes 25165824
  270.8 0.0 copy-done.2
  270.8 0.6 copy.15
  271.4 0.0 copy-done.1
  271.4 0.6 copy.16
Async XLA Ops:
  253.2 12.9 %copy-start = (bf16[3072,2048]{1,0:T(8,128)(2,1)S(1)}, bf16[3072,2048]{1,0:T(8,128)(2,1)}, u32[]{:S(2)}) copy-start(bf16[3072,2048]{1,0:T(8,128)(2,1)} %get-tuple-element.17) | copy-start | bytes 37748740
  266.1 4.8 %copy-start.2 = (f32[1,2048]{1,0:T(1,128)S(1)}, f32[1,2048]{1,0:T(1,128)}, u32[]{:S(2)}) copy-start(f32[1,2048]{1,0:T(1,128)} %get-tuple-element.10) | copy-start | bytes 24580
  266.1 5.4 %copy-start.1 = (f32[1,2048]{1,0:T(1,128)S(1)}, f32[1,2048]{1,0:T(1,128)}, u32[]{:S(2)}) copy-start(f32[1,2048]{1,0:T(1,128)} %get-tuple-element.11) | copy-start | bytes 24580
where the time goes:
time: 272 us
  Pallas kernels  253 us (93%)
  local copies, waits for them, and re-layouts  18.9 us (7%)
    pallas_call x1, Pallas kernels, serve(): pl.pallas_call(functools.partial(serve_kernel, n, chunks), out_shape=(who...  253 us
    unnamed x10, local copies, waits for them, and re-layouts  18.9 us

commit v1 on v0

--- a/solution.py
+++ b/solution.py
@@ -10,7 +10,7 @@
 keep_rate = 0.7
 MESH = pl.DeviceIdType.MESH
 CHUNKS = 4
-VMEM_LIMIT = 60 * 2**20
+VMEM_LIMIT = 36 * 2**20
 
 
 def ring_place(r, n):
@@ -30,7 +30,7 @@
 
 def serve_kernel(
     n, chunks, gain_ref, wg_ref, ag_ref, wu_ref, au_ref, go_ref, uo_ref, fg_ref, fu_ref,
-    w_in, fresh, narrow, gains, part, got, in_sem, max_send, max_recv, send_sem, recv_sem, own_sem,
+    w_in, fresh, gains, part, got, in_sem, max_send, max_recv, send_sem, recv_sem,
 ):
     me = lax.axis_index("rows")
     place = ring_place(me, n)
@@ -99,10 +99,10 @@
         owner = ring_row((place + turn) % n, n)
         return pl.ds(pl.multiple_of(owner * rows + c * size, size), size)
 
-    def send(way, step, c, first=False):
+    def send(way, step, c):
         at = here((n - step) if way == 0 else step, c)
         return pltpu.make_async_remote_copy(
-            src_ref=narrow.at[way, pl.ds(c * size, size)] if first else outs[way].at[at],
+            src_ref=outs[way].at[at],
             dst_ref=outs[way].at[at],
             send_sem=send_sem.at[way, step, c],
             recv_sem=recv_sem.at[way, step, c],
@@ -129,18 +129,11 @@
                 @pl.loop(0, size // 16)
                 def _(i):
                     at = pl.ds(pl.multiple_of(c * size + i * 16, 16), 16)
-                    narrow[way, at, :] = (fresh[way, at, :] * by).astype(jnp.bfloat16)
+                    to_at = pl.ds(pl.multiple_of(me * rows + c * size + i * 16, 16), 16)
+                    outs[way][to_at, :] = (fresh[way, at, :] * by).astype(jnp.bfloat16)
 
             if c:
-                send(way, 0, c - 1, True).start()
-    own = [
-        pltpu.make_async_copy(
-            narrow.at[way], outs[way].at[pl.ds(pl.multiple_of(me * rows, rows), rows)], own_sem.at[way]
-        )
-        for way in range(2)
-    ]
-    for copy in own:
-        copy.start()
+                send(way, 0, c - 1).start()
 
     @pl.loop(1, n - 1)
     def _(step):
@@ -153,11 +146,9 @@
         for way in range(2):
             landed(way, n - 2, c)
 
-    for copy in own:
-        copy.wait()
     for c in range(chunks):
         for way in range(2):
-            send(way, 0, c, True).wait_send()
+            send(way, 0, c).wait_send()
 
     @pl.loop(1, n - 1)
     def _(step):
@@ -171,7 +162,7 @@
     chunks = CHUNKS
     while rows % (16 * chunks):
         chunks -= 1
-    whole = jax.ShapeDtypeStruct((n * rows, columns), jnp.bfloat16)
+    whole = pltpu.VMEM((n * rows, columns), jnp.bfloat16)
     line = jax.ShapeDtypeStruct((1, columns), jnp.float32)
     anywhere = pl.BlockSpec(memory_space=pl.ANY)
     near = pl.BlockSpec(memory_space=pltpu.VMEM)
@@ -179,11 +170,10 @@
         functools.partial(serve_kernel, n, chunks),
         out_shape=(whole, whole, line, line),
         in_specs=[near] + [anywhere] * 4,
-        out_specs=(anywhere, anywhere, near, near),
+        out_specs=(near, near, near, near),
         scratch_shapes=[
             pltpu.VMEM((2, rows, columns), jnp.float32),
             pltpu.VMEM((2, rows, columns), jnp.float32),
-            pltpu.VMEM((2, rows, columns), jnp.bfloat16),
             pltpu.VMEM((rows, 128), jnp.float32),
             pltpu.VMEM((2, columns), jnp.float32),
             pltpu.VMEM((n - 1, 2, columns), jnp.float32),
@@ -192,7 +182,6 @@
             pltpu.SemaphoreType.DMA((n - 1,)),
             pltpu.SemaphoreType.DMA((2, n - 1, chunks)),
             pltpu.SemaphoreType.DMA((2, n - 1, chunks)),
-            pltpu.SemaphoreType.DMA((2,)),
         ],
         compiler_params=pltpu.CompilerParams(
             collective_id=0, has_side_effects=True, vmem_limit_bytes=VMEM_LIMIT
@@ -201,8 +190,38 @@
     )(norm_gain, w_gate, avg_gate, w_up, avg_up)
 
 
+def keep_kernel(parts, gate_ref, up_ref, go_ref, uo_ref, sem):
+    size = gate_ref.shape[0] // parts
+    copies = []
+    for c in range(parts):
+        at = pl.ds(c * size, size)
+        for k, (src, dst) in enumerate(((gate_ref, go_ref), (up_ref, uo_ref))):
+            copy = pltpu.make_async_copy(src.at[at], dst.at[at], sem.at[k, c])
+            copy.start()
+            copies.append(copy)
+    for copy in copies:
+        copy.wait()
+
+
+def keep(gate, up):
+    parts = 8
+    whole = jax.ShapeDtypeStruct(gate.shape, gate.dtype)
+    near = pl.BlockSpec(memory_space=pltpu.VMEM)
+    anywhere = pl.BlockSpec(memory_space=pl.ANY)
+    return pl.pallas_call(
+        functools.partial(keep_kernel, parts),
+        out_shape=(whole, whole),
+        in_specs=[near] * 2,
+        out_specs=(anywhere,) * 2,
+        scratch_shapes=[pltpu.SemaphoreType.DMA((2, parts))],
+        compiler_params=pltpu.CompilerParams(vmem_limit_bytes=2**20),
+        name="keep",
+    )(gate, up)
+
+
 def local(n, w_gate, avg_gate, w_up, avg_up, norm_gain):
     serve_gate, serve_up, factor_gate, factor_up = serve(w_gate, avg_gate, w_up, avg_up, norm_gain, n)
+    serve_gate, serve_up = keep(serve_gate, serve_up)
     return (serve_gate, serve_up, factor_gate[0], factor_up[0])
 
 

time: 272 us -> 263 us (0.967)
  local copies, waits for them, and re-layouts: 18.9 us -> 1.21 us
  Pallas kernels: 253 us -> 261 us
    unnamed x10 -> x6, local copies, waits for them, and re-layouts: 18.9 us -> 1.21 us
    pallas_call x0 -> x1, Pallas kernels: none -> 8.51 us  [keep(): pl.pallas_call(functools.partial(keep_kernel, parts), out_shape=(whole, w...]
where the time goes in v1:
time: 263 us
  Pallas kernels  261 us (99%)
    pallas_call x1, Pallas kernels, serve(): pl.pallas_call(functools.partial(serve_kernel, n, chunks), out_shape=(who...  252 us
    pallas_call x1, Pallas kernels, keep(): pl.pallas_call(functools.partial(keep_kernel, parts), out_shape=(whole, w...  8.51 us

profile of v1, /device:TPU:0, one launch (start us, length us, event | category | flops | bytes accessed | tf_op | source)
XLA Modules:
  0.0 262.8 jit_solution(16115067504691958641)
XLA Ops:
  0.6 252.4 %serve.1 = (bf16[3072,2048]{1,0:T(8,128)(2,1)S(1)}, bf16[3072,2048]{1,0:T(8,128)(2,1)S(1)}, f32[1,2048]{1,0:T(1,128)}, f32[1,2048]{1,0:T(1,128)}) custom-call(f32[384]{0:T(512)} %gain_ref.1, f32[384,2048]{1,0:T(8,128)} %wg_ref.1, f32[384,2048]{1,0:T(8,128)} %ag_ref.1, f32[384,2048]{1,0:T(8,128)} %wu_ref.1, f32[384,2048]{1,0:T(8,128)} %au_ref.1), custom_call_target="tpu_custom_call" | custom-call | tf_op jit(solution)/shard_map/serve/pallas_call | solution.py:169
  253.0 0.0 copy-start.1
  253.0 0.0 copy-start
  253.1 8.5 %keep.1 = (bf16[3072,2048]{1,0:T(8,128)(2,1)}, bf16[3072,2048]{1,0:T(8,128)(2,1)}) custom-call(bf16[3072,2048]{1,0:T(8,128)(2,1)S(1)} %get-tuple-element.10.gate_ref, bf16[3072,2048]{1,0:T(8,128)(2,1)S(1)} %get-tuple-element.11.up_ref), custom_call_target="tpu_custom_call" | custom-call | tf_op jit(solution)/shard_map/keep/pallas_call | solution.py:211
  261.6 0.0 copy-done.1
  261.6 0.6 copy.11
  262.2 0.0 copy-done
  262.2 0.6 copy.12
Async XLA Ops:
  253.0 8.5 %copy-start.1 = (f32[1,2048]{1,0:T(1,128)S(1)}, f32[1,2048]{1,0:T(1,128)}, u32[]{:S(2)}) copy-start(f32[1,2048]{1,0:T(1,128)} %get-tuple-element.14) | copy-start | bytes 24580
  253.0 9.1 %copy-start = (f32[1,2048]{1,0:T(1,128)S(1)}, f32[1,2048]{1,0:T(1,128)}, u32[]{:S(2)}) copy-start(f32[1,2048]{1,0:T(1,128)} %get-tuple-element.15) | copy-start | bytes 24580

commit v2 on v1

v2 whole, which is shorter than its diff:
```python
import functools

import jax
import jax.numpy as jnp
from jax import lax
from jax.experimental import pallas as pl
from jax.experimental.pallas import tpu as pltpu
from jax.sharding import PartitionSpec as P

keep_rate = 0.7
MESH = pl.DeviceIdType.MESH
PARTS = 2
TAIL = 1
SPLIT = 8
EARLY = 16
KEEP = 8
VMEM_LIMIT = 36 * 2**20


def ring_place(r, n):
    if n % 2:
        return r
    x, z = r % 2, r // 2
    return z + x * (n - 1 - 2 * z)


def ring_row(p, n):
    if n % 2:
        return p
    half = n // 2
    x, k = p // half, p % half
    return 2 * (k + x * (half - 1 - 2 * k)) + x


def serve_kernel(
    n, parts, gain_ref, wg_ref, ag_ref, wu_ref, au_ref,
    go_ref, uo_ref, fg_ref, fu_ref, gt_ref, ut_ref,
    w_in, fresh, early, gains, part, got,
    in_sem, max_send, max_recv, early_send, early_recv, send_sem, recv_sem, tail_sem,
):
    me = lax.axis_index("rows")
    place = ring_place(me, n)
    nxt = ring_row((place + 1) % n, n)
    prv = ring_row((place + n - 1) % n, n)
    rows, columns = wg_ref.shape
    half = rows // 2
    size = half // parts
    chunks = 2 * parts
    outs, to = (go_ref, uo_ref), (nxt, prv)
    ins = ((wg_ref, ag_ref), (wu_ref, au_ref))

    spans = [(0, way * half, size) for way in range(2)]
    spans += [(0, way * half + size, half - size) for way in range(2)]
    spans += [(1, way * half, half) for way in range(2)]
    for s, (k, first, count) in enumerate(spans):
        at = pl.ds(first, count)
        for j, dst in enumerate((w_in, fresh)):
            load = pltpu.make_async_copy(ins[k][j].at[at], dst.at[k, at], in_sem.at[s])
            load.start()

    barrier = pltpu.get_barrier_semaphore()
    for d in range(1, n):
        pl.semaphore_signal(barrier, inc=1, device_id={"rows": (me + d) % n}, device_id_type=MESH)

    for first in range(0, rows, 128):
        count = min(128, rows - first)
        line = gain_ref[first : first + count].reshape(1, count)
        gains[first : first + count, :] = jnp.broadcast_to(line, (128, count)).T

    def blend(s, top):
        k, first, count = spans[s]
        both = fresh.at[k, pl.ds(0, 2 * count)]
        pltpu.make_async_copy(both, both, in_sem.at[s]).wait()

        def body(i, top):
            at = pl.ds(pl.multiple_of(first + i * 8, 8), 8)
            gain = jnp.tile(gains[at, :], (1, columns // 128))
            value = (keep_rate * fresh[k, at, :] + (1.0 - keep_rate) * w_in[k, at, :]) * gain
            fresh[k, at, :] = value
            return jnp.maximum(top, jnp.abs(value))

        return lax.fori_loop(0, count // 8, body, top)

    cuts = ((0, SPLIT), (SPLIT, EARLY))

    def ahead(way, b):
        first, end = cuts[b]
        return pltpu.make_async_remote_copy(
            src_ref=fresh.at[0, pl.ds(way * half + first, end - first)],
            dst_ref=early.at[way, pl.ds(first, end - first)],
            send_sem=early_send.at[way],
            recv_sem=early_recv.at[way],
            device_id={"rows": to[way]},
            device_id_type=MESH,
        )

    def spread(k, top):
        part[k] = jnp.max(top, axis=0, keepdims=True)
        for d in range(1, n):
            pltpu.make_async_remote_copy(
                src_ref=part.at[k],
                dst_ref=got.at[k, d - 1],
                send_sem=max_send.at[k],
                recv_sem=max_recv.at[k],
                device_id={"rows": (me + d) % n},
                device_id_type=MESH,
            ).start()

    def drained(ref, sem):
        pltpu.make_async_copy(ref, ref, sem).wait()

    def gather(k, out):
        drained(got.at[k], max_recv.at[k])
        factor = part[k]
        for d in range(n - 1):
            factor = jnp.maximum(factor, got[k, d])
        out[...] = factor
        return 1.0 / factor

    top = jnp.zeros((8, columns), jnp.float32)
    top = blend(0, top)
    top = blend(1, top)
    pl.semaphore_wait(barrier, n - 1)
    for way in range(2):
        ahead(way, 0).start()
    top = blend(2, top)
    top = blend(3, top)
    spread(0, top)
    for way in range(2):
        ahead(way, 1).start()
    top = jnp.zeros((8, columns), jnp.float32)
    top = blend(4, top)
    top = blend(5, top)
    spread(1, top)

    def block(turn):
        return ring_row((place + turn) % n, n) * rows

    def turn_out(way, step):
        return (n - step) if way == 0 else step

    def turn_in(way, step):
        return (n - step - 1) if way == 0 else (step + 1)

    def moved(way, step, q, turn, skip=0):
        k, first = q // parts, way * half + (q % parts) * size + skip
        at = outs[k].at[pl.ds(pl.multiple_of(block(turn) + first, 16), size - skip)]
        return pltpu.make_async_remote_copy(
            src_ref=at,
            dst_ref=at,
            send_sem=send_sem.at[way],
            recv_sem=recv_sem.at[way, step, q],
            device_id={"rows": to[way]},
            device_id_type=MESH,
        )

    def send(way, step, q, skip=0):
        return moved(way, step, q, turn_out(way, step), skip)

    def landed(way, step, q, skip=0):
        moved(way, step, q, turn_in(way, step), skip).wait_recv()

    def narrow(k, scale, load, first, count, base):
        by = jnp.broadcast_to(scale, (16, columns))

        @pl.loop(0, count // 16)
        def _(i):
            to_at = pl.ds(pl.multiple_of(base + i * 16, 16), 16)
            outs[k][to_at, :] = (load(pl.ds(pl.multiple_of(first + i * 16, 16), 16)) * by).astype(jnp.bfloat16)

    pending = []
    for k in range(2):
        scale = gather(k, (fg_ref, fu_ref)[k])
        if k == 0:
            gate_scale = scale
        for p in range(parts):
            for way in range(2):
                skip = EARLY if k == 0 and p == 0 else 0
                first = way * half + p * size + skip
                if skip < size:
                    narrow(k, scale, lambda at: fresh[k, at, :], first, size - skip, block(0) + first)
                    pending.append(send(way, 0, k * parts + p, skip))
                if len(pending) > 1:
                    pending.pop(0).start()
    pending.pop(0).start()
    for way in range(2):
        drained(early.at[way], early_recv.at[way])
        narrow(0, gate_scale, lambda at: early[way, at, :], 0, EARLY, block(turn_in(way, 0)) + way * half)
    for way in range(2):
        narrow(0, gate_scale, lambda at: fresh[0, at, :], way * half, EARLY, block(0) + way * half)

    skips = [EARLY] + [0] * (chunks - 1)
    for q in range(chunks):
        for way in range(2):
            if skips[q] < size:
                landed(way, 0, q, skips[q])
            send(way, 1, q).start()

    @pl.loop(2, n - 2)
    def _(step):
        for q in range(chunks):
            for way in range(2):
                landed(way, step - 1, q)
                send(way, step, q).start()

    last = n - 2
    for q in range(TAIL):
        for way in range(2):
            landed(way, last - 1, q)
    tails = []
    for way, ref in enumerate((gt_ref, ut_ref)):
        at = pl.ds(pl.multiple_of(block(turn_out(way, last)) + way * half, 16), TAIL * size)
        copy = pltpu.make_async_copy(go_ref.at[at], ref, tail_sem.at[way])
        copy.start()
        tails.append(copy)
    for q in range(TAIL, chunks):
        for way in range(2):
            landed(way, last - 1, q)
            send(way, last, q).start()
    for copy in tails:
        copy.wait()

    for q in range(TAIL, chunks):
        for way in range(2):
            landed(way, last, q)
    for way in range(2):
        drained(early.at[way], early_send.at[way])
        drained(got.at[way], max_send.at[way])
        sent = go_ref.at[pl.ds(0, (n - 1) * rows - EARLY - TAIL * size)]
        drained(sent, send_sem.at[way])


def serve(w_gate, avg_gate, w_up, avg_up, norm_gain, n):
    rows, columns = w_gate.shape
    half = rows // 2
    parts = PARTS
    while half % (16 * parts):
        parts -= 1
    size = half // parts
    whole = pltpu.VMEM((n * rows, columns), jnp.bfloat16)
    tail = pltpu.HBM((TAIL * size, columns), jnp.bfloat16)
    line = pltpu.VMEM((1, columns), jnp.float32)
    anywhere = pl.BlockSpec(memory_space=pl.ANY)
    near = pl.BlockSpec(memory_space=pltpu.VMEM)
    return pl.pallas_call(
        functools.partial(serve_kernel, n, parts),
        out_shape=(whole, whole, line, line, tail, tail),
        in_specs=[near] + [anywhere] * 4,
        out_specs=(near, near, near, near, anywhere, anywhere),
        scratch_shapes=[
            pltpu.VMEM((2, rows, columns), jnp.float32),
            pltpu.VMEM((2, rows, columns), jnp.float32),
            pltpu.VMEM((2, EARLY, columns), jnp.float32),
            pltpu.VMEM((rows, 128), jnp.float32),
            pltpu.VMEM((2, 1, columns), jnp.float32),
            pltpu.VMEM((2, n - 1, 1, columns), jnp.float32),
            pltpu.SemaphoreType.DMA((6,)),
            pltpu.SemaphoreType.DMA((2,)),
            pltpu.SemaphoreType.DMA((2,)),
            pltpu.SemaphoreType.DMA((2,)),
            pltpu.SemaphoreType.DMA((2,)),
            pltpu.SemaphoreType.DMA((2,)),
            pltpu.SemaphoreType.DMA((2, n - 1, 2 * parts)),
            pltpu.SemaphoreType.DMA((2,)),
        ],
        compiler_params=pltpu.CompilerParams(
            collective_id=0, has_side_effects=True, vmem_limit_bytes=VMEM_LIMIT
        ),
        name="serve",
    )(norm_gain, w_gate, avg_gate, w_up, avg_up)


def keep_kernel(parts, gate_ref, up_ref, fg_ref, fu_ref, go_ref, uo_ref, fgo_ref, fuo_ref, lines, sem, line_sem):
    size = gate_ref.shape[0] // parts
    for c in range(parts):
        at = pl.ds(c * size, size)
        for k, (src, dst) in enumerate(((gate_ref, go_ref), (up_ref, uo_ref))):
            pltpu.make_async_copy(src.at[at], dst.at[at], sem.at[k]).start()
    for k, (src, dst) in enumerate(((fg_ref, fgo_ref), (fu_ref, fuo_ref))):
        lines[k][...] = src[0]
        pltpu.make_async_copy(lines[k], dst, line_sem.at[k]).start()
    for k, (ref, out, line) in enumerate(((gate_ref, go_ref, fgo_ref), (up_ref, uo_ref, fuo_ref))):
        pltpu.make_async_copy(ref, out, sem.at[k]).wait()
        pltpu.make_async_copy(lines[k], line, line_sem.at[k]).wait()


def keep(gate, up, factor_gate, factor_up):
    parts = KEEP
    columns = gate.shape[1]
    whole = jax.ShapeDtypeStruct(gate.shape, gate.dtype)
    line = jax.ShapeDtypeStruct((columns,), factor_gate.dtype)
    near = pl.BlockSpec(memory_space=pltpu.VMEM)
    anywhere = pl.BlockSpec(memory_space=pl.ANY)
    return pl.pallas_call(
        functools.partial(keep_kernel, parts),
        out_shape=(whole, whole, line, line),
        in_specs=[near] * 4,
        out_specs=(anywhere,) * 4,
        scratch_shapes=[
            [pltpu.VMEM((columns,), jnp.float32)] * 2,
            pltpu.SemaphoreType.DMA((2,)),
            pltpu.SemaphoreType.DMA((2,)),
        ],
        compiler_params=pltpu.CompilerParams(vmem_limit_bytes=2**20),
        cost_estimate=pl.CostEstimate(flops=100 * gate.size, bytes_accessed=4 * gate.size, transcendentals=0),
        name="keep",
    )(gate, up, factor_gate, factor_up)


def close_kernel(n, ahead_ref, back_ref, in_ref, out_ref, sem):
    place = ring_place(lax.axis_index("rows"), n)
    size = ahead_ref.shape[0]
    rows = out_ref.shape[0] // n
    copies = []
    for way, (src, turn) in enumerate(((ahead_ref, 1), (back_ref, n - 1))):
        first = ring_row((place + turn) % n, n) * rows + way * (rows // 2)
        copies.append(pltpu.make_async_copy(src, out_ref.at[pl.ds(pl.multiple_of(first, 16), size)], sem.at[way]))
        copies[-1].start()
    for copy in copies:
        copy.wait()


def close(n, ahead, back, gate):
    near = pl.BlockSpec(memory_space=pltpu.VMEM)
    anywhere = pl.BlockSpec(memory_space=pl.ANY)
    ahead, back = (pltpu.with_memory_space_constraint(t, pltpu.VMEM) for t in (ahead, back))
    return pl.pallas_call(
        functools.partial(close_kernel, n),
        out_shape=jax.ShapeDtypeStruct(gate.shape, gate.dtype),
        in_specs=[near, near, anywhere],
        out_specs=anywhere,
        scratch_shapes=[pltpu.SemaphoreType.DMA((2,))],
        input_output_aliases={2: 0},
        compiler_params=pltpu.CompilerParams(vmem_limit_bytes=2**20),
        name="close",
    )(ahead, back, gate)


def local(n, w_gate, avg_gate, w_up, avg_up, norm_gain):
    gate, up, factor_gate, factor_up, ahead, back = serve(w_gate, avg_gate, w_up, avg_up, norm_gain, n)
    ring = [ring_row(p, n) for p in range(n)]
    pairs = [(ring[p], ring[(p + 1) % n]) for p in range(n)]
    ahead = lax.ppermute(ahead, "rows", pairs)
    back = lax.ppermute(back, "rows", [(b, a) for a, b in pairs])
    gate, up, factor_gate, factor_up = keep(gate, up, factor_gate, factor_up)
    return (close(n, ahead, back, gate), up, factor_gate, factor_up)


def solution(mesh):
    placed = (P("rows", "width"),) * 4 + (P("rows"),)
    return jax.shard_map(
        functools.partial(local, mesh.shape["rows"]),
        mesh=mesh,
        in_specs=placed,
        out_specs=(P(None, "width"), P(None, "width"), P("width"), P("width")),
        check_vma=False,
    )
```

time: 263 us -> 252 us (0.958)
  Pallas kernels: 261 us -> 249 us
    pallas_call x1 -> x2, Pallas kernels: 252 us -> 240 us  [the longest x1 240 us: serve(): pl.pallas_call(functools.partial(serve_kernel, n, parts), out_shape=(whol...]
  transfers between devices with their start and end apart: 0 -> 2, of which waited for: 0 -> 1; matrix products, arithmetic and copies ran while one was open for 0% -> 0% of each run, Pallas kernels for 0% -> 3%
where the time goes in v2:
time: 252 us
  Pallas kernels  249 us (99%)
    pallas_call x1, Pallas kernels, serve(): pl.pallas_call(functools.partial(serve_kernel, n, parts), out_shape=(whol...  240 us
    pallas_call x1, Pallas kernels, keep(): pl.pallas_call(functools.partial(keep_kernel, parts), out_shape=(whole, w...  8.41 us
  transfers between devices with their start and end apart: 2, of which 1 were waited for; matrix products, arithmetic and copies ran while one was open for 0% of the time, Pallas kernels for 3%

profile of v2, /device:TPU:0, one launch (start us, length us, event | category | flops | bytes accessed | tf_op | source)
XLA Modules:
  0.0 252.0 jit_solution(14521875749094826085)
XLA Ops:
  0.6 239.6 %serve.1 = (bf16[3072,2048]{1,0:T(8,128)(2,1)S(1)}, bf16[3072,2048]{1,0:T(8,128)(2,1)S(1)}, f32[1,2048]{1,0:T(1,128)S(1)}, f32[1,2048]{1,0:T(1,128)S(1)}, bf16[9...) custom-call(f32[384]{0:T(512)} %gain_ref.1, f32[384,2048]{1,0:T(8,128)} %wg_ref.1, f32[384,2048]{1,0:T(8,128)} %ag_ref.1, ...), custom_call_target="tpu_custom_call" | custom-call | tf_op jit(solution)/shard_map/serve/pallas_call | solution.py:245
  240.2 1.3 collective-permute-start
  241.5 0.8 collective-permute-start.1
  242.3 8.4 %keep.1 = (bf16[3072,2048]{1,0:T(8,128)(2,1)}, bf16[3072,2048]{1,0:T(8,128)(2,1)}, f32[2048]{0:T(1024)}, f32[2048]{0:T(1024)}) custom-call(bf16[3072,2048]{1,0:T(8,128)(2,1)S(1)} %get-tuple-element.16.gate_ref, bf16[3072,2048]{1,0:T(8,128)(2,1)S(1)} %get-tuple-element.17.up_ref, f32[1,2048]{1,0:T(1,128)S(1)} %get-tuple-element.18.fg_ref, ...), custom_call_target="tpu_custom_call" | custom-call | flops 629145600 | bytes 25165824 | tf_op jit(solution)/shard_map/keep/pallas_call | solution.py:294
  250.7 0.0 collective-permute-done.ahead_ref
  250.7 0.4 collective-permute-done.1.back_ref
  251.1 0.9 close.1
Async XLA Ops:
  240.2 10.5 %collective-permute-start = (bf16[96,2048]{1,0:T(8,128)(2,1)}, bf16[96,2048]{1,0:T(8,128)(2,1)S(1)}, u32[]{:S(2)}, u32[]{:S(2)}) collective-permute-start(bf16[96,2048]{1,0:T(8,128)(2,1)} %get-tuple-element.14), channel_id=1, source_target_pairs={{0,8},{8,16},{16,24},{24,28},{28,20},{20,12},{12,4},{4,0},{1,9},{9... | collective-permute-start | bytes 1179656 | tf_op jit(solution)/shard_map/ppermute | solution.py:343
  241.5 9.6 %collective-permute-start.1 = (bf16[96,2048]{1,0:T(8,128)(2,1)}, bf16[96,2048]{1,0:T(8,128)(2,1)S(1)}, u32[]{:S(2)}, u32[]{:S(2)}) collective-permute-start(bf16[96,2048]{1,0:T(8,128)(2,1)} %get-tuple-element.15), channel_id=1, source_target_pairs={{8,0},{16,8},{24,16},{28,24},{20,28},{12,20},{4,12},{0,4},{9,1},{1... | collective-permute-start | bytes 1179656 | tf_op jit(solution)/shard_map/ppermute | solution.py:344

commit v3 on v2

--- a/solution.py
+++ b/solution.py
@@ -9,10 +9,10 @@
 
 keep_rate = 0.7
 MESH = pl.DeviceIdType.MESH
-PARTS = 2
-TAIL = 1
-SPLIT = 8
+TAIL = 112
+SPLIT = 16
 EARLY = 16
+FIRST = 16
 KEEP = 8
 VMEM_LIMIT = 36 * 2**20
 
@@ -33,24 +33,26 @@
 
 
 def serve_kernel(
-    n, parts, gain_ref, wg_ref, ag_ref, wu_ref, au_ref,
+    n, size, gain_ref, wg_ref, ag_ref, wu_ref, au_ref,
     go_ref, uo_ref, fg_ref, fu_ref, gt_ref, ut_ref,
     w_in, fresh, early, gains, part, got,
     in_sem, max_send, max_recv, early_send, early_recv, send_sem, recv_sem, tail_sem,
 ):
     me = lax.axis_index("rows")
+    barrier = pltpu.get_barrier_semaphore()
+    for d in range(1, n):
+        pl.semaphore_signal(barrier, inc=1, device_id={"rows": (me + d) % n}, device_id_type=MESH)
+
     place = ring_place(me, n)
     nxt = ring_row((place + 1) % n, n)
     prv = ring_row((place + n - 1) % n, n)
     rows, columns = wg_ref.shape
     half = rows // 2
-    size = half // parts
-    chunks = 2 * parts
     outs, to = (go_ref, uo_ref), (nxt, prv)
     ins = ((wg_ref, ag_ref), (wu_ref, au_ref))
 
-    spans = [(0, way * half, size) for way in range(2)]
-    spans += [(0, way * half + size, half - size) for way in range(2)]
+    spans = [(0, way * half, FIRST) for way in range(2)]
+    spans += [(0, way * half + FIRST, half - FIRST) for way in range(2)]
     spans += [(1, way * half, half) for way in range(2)]
     for s, (k, first, count) in enumerate(spans):
         at = pl.ds(first, count)
@@ -58,10 +60,6 @@
             load = pltpu.make_async_copy(ins[k][j].at[at], dst.at[k, at], in_sem.at[s])
             load.start()
 
-    barrier = pltpu.get_barrier_semaphore()
-    for d in range(1, n):
-        pl.semaphore_signal(barrier, inc=1, device_id={"rows": (me + d) % n}, device_id_type=MESH)
-
     for first in range(0, rows, 128):
         count = min(128, rows - first)
         line = gain_ref[first : first + count].reshape(1, count)
@@ -69,7 +67,7 @@
 
     def blend(s, top):
         k, first, count = spans[s]
-        both = fresh.at[k, pl.ds(0, 2 * count)]
+        both = fresh.at[:, pl.ds(0, count)]
         pltpu.make_async_copy(both, both, in_sem.at[s]).wait()
 
         def body(i, top):
@@ -81,7 +79,7 @@
 
         return lax.fori_loop(0, count // 8, body, top)
 
-    cuts = ((0, SPLIT), (SPLIT, EARLY))
+    cuts = ((0, SPLIT),)
 
     def ahead(way, b):
         first, end = cuts[b]
@@ -126,13 +124,14 @@
     top = blend(2, top)
     top = blend(3, top)
     spread(0, top)
-    for way in range(2):
-        ahead(way, 1).start()
     top = jnp.zeros((8, columns), jnp.float32)
     top = blend(4, top)
     top = blend(5, top)
     spread(1, top)
 
+    pieces = [(k, first, count) for k in range(2) for first, count in ((0, size), (size, half - size))]
+    chunks = len(pieces)
+
     def block(turn):
         return ring_row((place + turn) % n, n) * rows
 
@@ -143,8 +142,9 @@
         return (n - step - 1) if way == 0 else (step + 1)
 
     def moved(way, step, q, turn, skip=0):
-        k, first = q // parts, way * half + (q % parts) * size + skip
-        at = outs[k].at[pl.ds(pl.multiple_of(block(turn) + first, 16), size - skip)]
+        k, first, count = pieces[q]
+        first += way * half + skip
+        at = outs[k].at[pl.ds(pl.multiple_of(block(turn) + first, 16), count - skip)]
         return pltpu.make_async_remote_copy(
             src_ref=at,
             dst_ref=at,
@@ -168,32 +168,28 @@
             to_at = pl.ds(pl.multiple_of(base + i * 16, 16), 16)
             outs[k][to_at, :] = (load(pl.ds(pl.multiple_of(first + i * 16, 16), 16)) * by).astype(jnp.bfloat16)
 
+    skips = [EARLY] + [0] * (chunks - 1)
     pending = []
-    for k in range(2):
-        scale = gather(k, (fg_ref, fu_ref)[k])
-        if k == 0:
-            gate_scale = scale
-        for p in range(parts):
-            for way in range(2):
-                skip = EARLY if k == 0 and p == 0 else 0
-                first = way * half + p * size + skip
-                if skip < size:
-                    narrow(k, scale, lambda at: fresh[k, at, :], first, size - skip, block(0) + first)
-                    pending.append(send(way, 0, k * parts + p, skip))
-                if len(pending) > 1:
-                    pending.pop(0).start()
+    scales = []
+    for q, (k, first, count) in enumerate(pieces):
+        if k == len(scales):
+            scales.append(gather(k, (fg_ref, fu_ref)[k]))
+        for way in range(2):
+            at = way * half + first + skips[q]
+            narrow(k, scales[k], lambda at: fresh[k, at, :], at, count - skips[q], block(0) + at)
+            pending.append(send(way, 0, q, skips[q]))
+            if len(pending) > 1:
+                pending.pop(0).start()
     pending.pop(0).start()
     for way in range(2):
         drained(early.at[way], early_recv.at[way])
-        narrow(0, gate_scale, lambda at: early[way, at, :], 0, EARLY, block(turn_in(way, 0)) + way * half)
-    for way in range(2):
-        narrow(0, gate_scale, lambda at: fresh[0, at, :], way * half, EARLY, block(0) + way * half)
-
-    skips = [EARLY] + [0] * (chunks - 1)
+        narrow(0, scales[0], lambda at: early[way, at, :], 0, EARLY, block(turn_in(way, 0)) + way * half)
+    for way in range(2):
+        narrow(0, scales[0], lambda at: fresh[0, at, :], way * half, EARLY, block(0) + way * half)
+
     for q in range(chunks):
         for way in range(2):
-            if skips[q] < size:
-                landed(way, 0, q, skips[q])
+            landed(way, 0, q, skips[q])
             send(way, 1, q).start()
 
     @pl.loop(2, n - 2)
@@ -204,46 +200,42 @@
                 send(way, step, q).start()
 
     last = n - 2
-    for q in range(TAIL):
-        for way in range(2):
-            landed(way, last - 1, q)
+    for way in range(2):
+        landed(way, last - 1, 0)
     tails = []
     for way, ref in enumerate((gt_ref, ut_ref)):
-        at = pl.ds(pl.multiple_of(block(turn_out(way, last)) + way * half, 16), TAIL * size)
+        at = pl.ds(pl.multiple_of(block(turn_out(way, last)) + way * half, 16), size)
         copy = pltpu.make_async_copy(go_ref.at[at], ref, tail_sem.at[way])
         copy.start()
         tails.append(copy)
-    for q in range(TAIL, chunks):
+    for q in range(1, chunks):
         for way in range(2):
             landed(way, last - 1, q)
             send(way, last, q).start()
     for copy in tails:
         copy.wait()
 
-    for q in range(TAIL, chunks):
+    for q in range(1, chunks):
         for way in range(2):
             landed(way, last, q)
     for way in range(2):
         drained(early.at[way], early_send.at[way])
         drained(got.at[way], max_send.at[way])
-        sent = go_ref.at[pl.ds(0, (n - 1) * rows - EARLY - TAIL * size)]
+        sent = go_ref.at[pl.ds(0, (n - 1) * rows - EARLY - size)]
         drained(sent, send_sem.at[way])
 
 
 def serve(w_gate, avg_gate, w_up, avg_up, norm_gain, n):
     rows, columns = w_gate.shape
     half = rows // 2
-    parts = PARTS
-    while half % (16 * parts):
-        parts -= 1
-    size = half // parts
+    size = min(TAIL, half // 32 * 16 + 16)
     whole = pltpu.VMEM((n * rows, columns), jnp.bfloat16)
-    tail = pltpu.HBM((TAIL * size, columns), jnp.bfloat16)
+    tail = pltpu.HBM((size, columns), jnp.bfloat16)
     line = pltpu.VMEM((1, columns), jnp.float32)
     anywhere = pl.BlockSpec(memory_space=pl.ANY)
     near = pl.BlockSpec(memory_space=pltpu.VMEM)
     return pl.pallas_call(
-        functools.partial(serve_kernel, n, parts),
+        functools.partial(serve_kernel, n, size),
         out_shape=(whole, whole, line, line, tail, tail),
         in_specs=[near] + [anywhere] * 4,
         out_specs=(near, near, near, near, anywhere, anywhere),
@@ -260,7 +252,7 @@
             pltpu.SemaphoreType.DMA((2,)),
             pltpu.SemaphoreType.DMA((2,)),
             pltpu.SemaphoreType.DMA((2,)),
-            pltpu.SemaphoreType.DMA((2, n - 1, 2 * parts)),
+            pltpu.SemaphoreType.DMA((2, n - 1, 4)),
             pltpu.SemaphoreType.DMA((2,)),
         ],
         compiler_params=pltpu.CompilerParams(

time: 252 us -> 252 us (level)
  transfers between devices with their start and end apart: 2 -> 2, of which waited for: 1 -> 2; matrix products, arithmetic and copies ran while one was open for 0% -> 0% of each run, Pallas kernels for 3% -> 3%
where the time goes in v3:
time: 252 us
  Pallas kernels  248 us (98%)
    pallas_call x1, Pallas kernels, serve(): pl.pallas_call(functools.partial(serve_kernel, n, size), out_shape=(whole...  238 us
    pallas_call x1, Pallas kernels, keep(): pl.pallas_call(functools.partial(keep_kernel, parts), out_shape=(whole, w...  8.41 us
  transfers between devices with their start and end apart: 2, of which 2 were waited for; matrix products, arithmetic and copies ran while one was open for 0% of the time, Pallas kernels for 3%

profile of v3, /device:TPU:0, one launch (start us, length us, event | category | flops | bytes accessed | tf_op | source)
XLA Modules:
  0.0 251.6 jit_solution(14769217296459223052)
XLA Ops:
  0.6 238.3 %serve.1 = (bf16[3072,2048]{1,0:T(8,128)(2,1)S(1)}, bf16[3072,2048]{1,0:T(8,128)(2,1)S(1)}, f32[1,2048]{1,0:T(1,128)S(1)}, f32[1,2048]{1,0:T(1,128)S(1)}, bf16[1...) custom-call(f32[384]{0:T(512)} %gain_ref.1, f32[384,2048]{1,0:T(8,128)} %wg_ref.1, f32[384,2048]{1,0:T(8,128)} %ag_ref.1, ...), custom_call_target="tpu_custom_call" | custom-call | tf_op jit(solution)/shard_map/serve/pallas_call | solution.py:237
  239.0 1.2 collective-permute-start
  240.1 0.9 collective-permute-start.1
  241.0 8.4 %keep.1 = (bf16[3072,2048]{1,0:T(8,128)(2,1)}, bf16[3072,2048]{1,0:T(8,128)(2,1)}, f32[2048]{0:T(1024)}, f32[2048]{0:T(1024)}) custom-call(bf16[3072,2048]{1,0:T(8,128)(2,1)S(1)} %get-tuple-element.16.gate_ref, bf16[3072,2048]{1,0:T(8,128)(2,1)S(1)} %get-tuple-element.17.up_ref, f32[1,2048]{1,0:T(1,128)S(1)} %get-tuple-element.18.fg_ref, ...), custom_call_target="tpu_custom_call" | custom-call | flops 629145600 | bytes 25165824 | tf_op jit(solution)/shard_map/keep/pallas_call | solution.py:286
  249.5 0.4 collective-permute-done.ahead_ref
  249.8 0.8 collective-permute-done.1.back_ref
  250.7 0.9 close.1
Async XLA Ops:
  239.0 10.9 %collective-permute-start = (bf16[112,2048]{1,0:T(8,128)(2,1)}, bf16[112,2048]{1,0:T(8,128)(2,1)S(1)}, u32[]{:S(2)}, u32[]{:S(2)}) collective-permute-start(bf16[112,2048]{1,0:T(8,128)(2,1)} %get-tuple-element.14), channel_id=1, source_target_pairs={{0,8},{8,16},{16,24},{24,28},{28,20},{20,12},{12,4},{4,0},{1,9},{9... | collective-permute-start | bytes 1376264 | tf_op jit(solution)/shard_map/ppermute | solution.py:335
  240.1 10.5 %collective-permute-start.1 = (bf16[112,2048]{1,0:T(8,128)(2,1)}, bf16[112,2048]{1,0:T(8,128)(2,1)S(1)}, u32[]{:S(2)}, u32[]{:S(2)}) collective-permute-start(bf16[112,2048]{1,0:T(8,128)(2,1)} %get-tuple-element.15), channel_id=1, source_target_pairs={{8,0},{16,8},{24,16},{28,24},{20,28},{12,20},{4,12},{0,4},{9,1},{1... | collective-permute-start | bytes 1376264 | tf_op jit(solution)/shard_map/ppermute | solution.py:336

commit v4 on v3

--- a/solution.py
+++ b/solution.py
@@ -13,7 +13,7 @@
 SPLIT = 16
 EARLY = 16
 FIRST = 16
-KEEP = 8
+KEEP = 16
 VMEM_LIMIT = 36 * 2**20
 
 
@@ -299,33 +299,29 @@
     )(gate, up, factor_gate, factor_up)
 
 
-def close_kernel(n, ahead_ref, back_ref, in_ref, out_ref, sem):
+def close_kernel(n, way, tail_ref, in_ref, out_ref, sem):
     place = ring_place(lax.axis_index("rows"), n)
-    size = ahead_ref.shape[0]
     rows = out_ref.shape[0] // n
-    copies = []
-    for way, (src, turn) in enumerate(((ahead_ref, 1), (back_ref, n - 1))):
-        first = ring_row((place + turn) % n, n) * rows + way * (rows // 2)
-        copies.append(pltpu.make_async_copy(src, out_ref.at[pl.ds(pl.multiple_of(first, 16), size)], sem.at[way]))
-        copies[-1].start()
-    for copy in copies:
-        copy.wait()
-
-
-def close(n, ahead, back, gate):
+    first = ring_row((place + (1, n - 1)[way]) % n, n) * rows + way * (rows // 2)
+    at = pl.ds(pl.multiple_of(first, 16), tail_ref.shape[0])
+    copy = pltpu.make_async_copy(tail_ref, out_ref.at[at], sem)
+    copy.start()
+    copy.wait()
+
+
+def close(n, way, tail, gate):
     near = pl.BlockSpec(memory_space=pltpu.VMEM)
     anywhere = pl.BlockSpec(memory_space=pl.ANY)
-    ahead, back = (pltpu.with_memory_space_constraint(t, pltpu.VMEM) for t in (ahead, back))
     return pl.pallas_call(
-        functools.partial(close_kernel, n),
+        functools.partial(close_kernel, n, way),
         out_shape=jax.ShapeDtypeStruct(gate.shape, gate.dtype),
-        in_specs=[near, near, anywhere],
+        in_specs=[near, anywhere],
         out_specs=anywhere,
-        scratch_shapes=[pltpu.SemaphoreType.DMA((2,))],
-        input_output_aliases={2: 0},
+        scratch_shapes=[pltpu.SemaphoreType.DMA],
+        input_output_aliases={1: 0},
         compiler_params=pltpu.CompilerParams(vmem_limit_bytes=2**20),
         name="close",
-    )(ahead, back, gate)
+    )(pltpu.with_memory_space_constraint(tail, pltpu.VMEM), gate)
 
 
 def local(n, w_gate, avg_gate, w_up, avg_up, norm_gain):
@@ -335,7 +331,7 @@
     ahead = lax.ppermute(ahead, "rows", pairs)
     back = lax.ppermute(back, "rows", [(b, a) for a, b in pairs])
     gate, up, factor_gate, factor_up = keep(gate, up, factor_gate, factor_up)
-    return (close(n, ahead, back, gate), up, factor_gate, factor_up)
+    return (close(n, 1, back, close(n, 0, ahead, gate)), up, factor_gate, factor_up)
 
 
 def solution(mesh):

time: 252 us -> 252 us (level)
  transfers between devices with their start and end apart: 2 -> 2, of which waited for: 2 -> 1; matrix products, arithmetic and copies ran while one was open for 0% -> 0% of each run, Pallas kernels for 3% -> 4%
where the time goes in v4:
time: 252 us; the launch traced here: 251 us
  Pallas kernels  248 us (98%)
    pallas_call x1, Pallas kernels, serve(): pl.pallas_call(functools.partial(serve_kernel, n, size), out_shape=(whole...  238 us
    pallas_call x1, Pallas kernels, keep(): pl.pallas_call(functools.partial(keep_kernel, parts), out_shape=(whole, w...  8.38 us
  transfers between devices with their start and end apart: 2, of which 1 were waited for; matrix products, arithmetic and copies ran while one was open for 0% of the time, Pallas kernels for 4%

profile of v4, /device:TPU:0, one launch (start us, length us, event | category | flops | bytes accessed | tf_op | source)
XLA Modules:
  0.0 251.4 jit_solution(2816435613206989436)
XLA Ops:
  0.6 238.3 %serve.1 = (bf16[3072,2048]{1,0:T(8,128)(2,1)S(1)}, bf16[3072,2048]{1,0:T(8,128)(2,1)S(1)}, f32[1,2048]{1,0:T(1,128)S(1)}, f32[1,2048]{1,0:T(1,128)S(1)}, bf16[1...) custom-call(f32[384]{0:T(512)} %gain_ref.1, f32[384,2048]{1,0:T(8,128)} %wg_ref.1, f32[384,2048]{1,0:T(8,128)} %ag_ref.1, ...), custom_call_target="tpu_custom_call" | custom-call | tf_op jit(solution)/shard_map/serve/pallas_call | solution.py:237
  239.0 1.2 collective-permute-start.1
  240.1 0.9 collective-permute-start
  241.0 8.4 %keep.1 = (bf16[3072,2048]{1,0:T(8,128)(2,1)}, bf16[3072,2048]{1,0:T(8,128)(2,1)}, f32[2048]{0:T(1024)}, f32[2048]{0:T(1024)}) custom-call(bf16[3072,2048]{1,0:T(8,128)(2,1)S(1)} %get-tuple-element.16.gate_ref, bf16[3072,2048]{1,0:T(8,128)(2,1)S(1)} %get-tuple-element.17.up_ref, f32[1,2048]{1,0:T(1,128)S(1)} %get-tuple-element.18.fg_ref, ...), custom_call_target="tpu_custom_call" | custom-call | flops 629145600 | bytes 25165824 | tf_op jit(solution)/shard_map/keep/pallas_call | solution.py:286
  249.4 0.4 collective-permute-done.1.tail_ref
  249.8 0.8 close.2.in_ref
  250.6 0.0 collective-permute-done.tail_ref
  250.7 0.8 close.3
Async XLA Ops:
  239.0 10.9 %collective-permute-start.1 = (bf16[112,2048]{1,0:T(8,128)(2,1)}, bf16[112,2048]{1,0:T(8,128)(2,1)S(1)}, u32[]{:S(2)}, u32[]{:S(2)}) collective-permute-start(bf16[112,2048]{1,0:T(8,128)(2,1)} %get-tuple-element.15), channel_id=1, source_target_pairs={{0,8},{8,16},{16,24},{24,28},{28,20},{20,12},{12,4},{4,0},{1,9},{9... | collective-permute-start | bytes 1376264 | tf_op jit(solution)/shard_map/ppermute | solution.py:331
  240.1 10.5 %collective-permute-start = (bf16[112,2048]{1,0:T(8,128)(2,1)}, bf16[112,2048]{1,0:T(8,128)(2,1)S(1)}, u32[]{:S(2)}, u32[]{:S(2)}) collective-permute-start(bf16[112,2048]{1,0:T(8,128)(2,1)} %get-tuple-element.14), channel_id=1, source_target_pairs={{8,0},{16,8},{24,16},{28,24},{20,28},{12,20},{4,12},{0,4},{9,1},{1... | collective-permute-start | bytes 1376264 | tf_op jit(solution)/shard_map/ppermute | solution.py:332

commit v5 on v4

--- a/solution.py
+++ b/solution.py
@@ -36,7 +36,7 @@
     n, size, gain_ref, wg_ref, ag_ref, wu_ref, au_ref,
     go_ref, uo_ref, fg_ref, fu_ref, gt_ref, ut_ref,
     w_in, fresh, early, gains, part, got,
-    in_sem, max_send, max_recv, early_send, early_recv, send_sem, recv_sem, tail_sem,
+    in_sem, max_send, max_recv, early_send, early_recv, send_sem, recv_sem,
 ):
     me = lax.axis_index("rows")
     barrier = pltpu.get_barrier_semaphore()
@@ -202,18 +202,18 @@
     last = n - 2
     for way in range(2):
         landed(way, last - 1, 0)
-    tails = []
     for way, ref in enumerate((gt_ref, ut_ref)):
-        at = pl.ds(pl.multiple_of(block(turn_out(way, last)) + way * half, 16), size)
-        copy = pltpu.make_async_copy(go_ref.at[at], ref, tail_sem.at[way])
-        copy.start()
-        tails.append(copy)
+        base = block(turn_out(way, last)) + way * half
+
+        @pl.loop(0, size // 16)
+        def _(i):
+            at = pl.ds(pl.multiple_of(base + i * 16, 16), 16)
+            ref[pl.ds(pl.multiple_of(i * 16, 16), 16), :] = go_ref[at, :]
+
     for q in range(1, chunks):
         for way in range(2):
             landed(way, last - 1, q)
             send(way, last, q).start()
-    for copy in tails:
-        copy.wait()
 
     for q in range(1, chunks):
         for way in range(2):
@@ -230,7 +230,7 @@
     half = rows // 2
     size = min(TAIL, half // 32 * 16 + 16)
     whole = pltpu.VMEM((n * rows, columns), jnp.bfloat16)
-    tail = pltpu.HBM((size, columns), jnp.bfloat16)
+    tail = pltpu.VMEM((size, columns), jnp.bfloat16)
     line = pltpu.VMEM((1, columns), jnp.float32)
     anywhere = pl.BlockSpec(memory_space=pl.ANY)
     near = pl.BlockSpec(memory_space=pltpu.VMEM)
@@ -238,7 +238,7 @@
         functools.partial(serve_kernel, n, size),
         out_shape=(whole, whole, line, line, tail, tail),
         in_specs=[near] + [anywhere] * 4,
-        out_specs=(near, near, near, near, anywhere, anywhere),
+        out_specs=(near,) * 6,
         scratch_shapes=[
             pltpu.VMEM((2, rows, columns), jnp.float32),
             pltpu.VMEM((2, rows, columns), jnp.float32),
@@ -253,7 +253,6 @@
             pltpu.SemaphoreType.DMA((2,)),
             pltpu.SemaphoreType.DMA((2,)),
             pltpu.SemaphoreType.DMA((2, n - 1, 4)),
-            pltpu.SemaphoreType.DMA((2,)),
         ],
         compiler_params=pltpu.CompilerParams(
             collective_id=0, has_side_effects=True, vmem_limit_bytes=VMEM_LIMIT

time: 252 us -> 251 us (level)
  no operation moved by 1% of the time
where the time goes in v5:
time: 251 us
  Pallas kernels  248 us (99%)
    pallas_call x1, Pallas kernels, serve(): pl.pallas_call(functools.partial(serve_kernel, n, size), out_shape=(whole...  238 us
    pallas_call x1, Pallas kernels, keep(): pl.pallas_call(functools.partial(keep_kernel, parts), out_shape=(whole, w...  8.38 us
  transfers between devices with their start and end apart: 2, of which 1 were waited for; matrix products, arithmetic and copies ran while one was open for 0% of the time, Pallas kernels for 4%

profile of v5, /device:TPU:0, one launch (start us, length us, event | category | flops | bytes accessed | tf_op | source)
XLA Modules:
  0.0 251.2 jit_solution(13781170763763359029)
XLA Ops:
  0.6 238.3 %serve.1 = (bf16[3072,2048]{1,0:T(8,128)(2,1)S(1)}, bf16[3072,2048]{1,0:T(8,128)(2,1)S(1)}, f32[1,2048]{1,0:T(1,128)S(1)}, f32[1,2048]{1,0:T(1,128)S(1)}, bf16[1...) custom-call(f32[384]{0:T(512)} %gain_ref.1, f32[384,2048]{1,0:T(8,128)} %wg_ref.1, f32[384,2048]{1,0:T(8,128)} %ag_ref.1, ...), custom_call_target="tpu_custom_call" | custom-call | tf_op jit(solution)/shard_map/serve/pallas_call | solution.py:237
  238.9 1.2 collective-permute-start.1
  240.1 0.9 collective-permute-start
  241.0 8.4 %keep.1 = (bf16[3072,2048]{1,0:T(8,128)(2,1)}, bf16[3072,2048]{1,0:T(8,128)(2,1)}, f32[2048]{0:T(1024)}, f32[2048]{0:T(1024)}) custom-call(bf16[3072,2048]{1,0:T(8,128)(2,1)S(1)} %get-tuple-element.16.gate_ref, bf16[3072,2048]{1,0:T(8,128)(2,1)S(1)} %get-tuple-element.17.up_ref, f32[1,2048]{1,0:T(1,128)S(1)} %get-tuple-element.18.fg_ref, ...), custom_call_target="tpu_custom_call" | custom-call | flops 629145600 | bytes 25165824 | tf_op jit(solution)/shard_map/keep/pallas_call | solution.py:285
  249.4 0.2 collective-permute-done.1.tail_ref
  249.6 0.8 close.2.in_ref
  250.4 0.0 collective-permute-done.tail_ref
  250.4 0.8 close.3
Async XLA Ops:
  238.9 10.7 %collective-permute-start.1 = (bf16[112,2048]{1,0:T(8,128)(2,1)S(1)}, bf16[112,2048]{1,0:T(8,128)(2,1)S(1)}, u32[]{:S(2)}, u32[]{:S(2)}) collective-permute-start(bf16[112,2048]{1,0:T(8,128)(2,1)S(1)} %get-tuple-element.15), channel_id=1, source_target_pairs={{0,8},{8,16},{16,24},{24,28},{28,20},{20,12},{12,4},{4,0},{1,9},{9... | collective-permute-start | bytes 1376264 | tf_op jit(solution)/shard_map/ppermute | solution.py:330
  240.1 10.3 %collective-permute-start = (bf16[112,2048]{1,0:T(8,128)(2,1)S(1)}, bf16[112,2048]{1,0:T(8,128)(2,1)S(1)}, u32[]{:S(2)}, u32[]{:S(2)}) collective-permute-start(bf16[112,2048]{1,0:T(8,128)(2,1)S(1)} %get-tuple-element.14), channel_id=1, source_target_pairs={{8,0},{16,8},{24,16},{28,24},{20,28},{12,20},{4,12},{0,4},{9,1},{1... | collective-permute-start | bytes 1376264 | tf_op jit(solution)/shard_map/ppermute | solution.py:331
